TPU v7x, 32 devices: a whole 2x2x4 slice. The times are simulated.
32 devices in a mesh: expert: 8 (over y, x, core), shard: 4 (over z).
Axes of the slice: x: 2, y: 2, z: 4, core: 2. Of those that a mesh axis runs over, the one named last changes fastest.
Arguments:
- w_gate: float32 [64, 2048, 1024], P('expert', 'shard'), may hold values from -0.1875 to 0.1875
- avg_gate: float32 [64, 2048, 1024], P('expert', 'shard'), may hold values from -0.125 to 0.125
- w_up: float32 [64, 2048, 1024], P('expert', 'shard'), may hold values from -0.1875 to 0.1875
- avg_up: float32 [64, 2048, 1024], P('expert', 'shard'), may hold values from -0.125 to 0.125
- mix_share: float32 [64], P('expert'), may hold values from 0.2 to 0.8
- router_weight: float32 [2048, 64], P('shard', 'expert'), may hold values from -0.125 to 0.125
- router_gain: float32 [2048], P('shard'), may hold values from 0.25 to 1.75
Outputs:
- serve_gate: bfloat16 [64, 2048, 1024], P('expert')
- serve_up: bfloat16 [64, 2048, 1024], P('expert')
- scale_gate: float32 [64, 1024], P('expert')
- scale_up: float32 [64, 1024], P('expert')
- serve_router: bfloat16 [2048, 64], replicated
All inputs are finite; a program needn't handle non-finite values.
Results may differ from a plain program's by a relative error of at most 0.001.
Values may be sent and summed in bfloat16 or wider, within the bound.
A program may use at most 256 MiB of HBM per device.

v0:
```python
import jax
import jax.numpy as jnp
from jax import lax
from jax.sharding import PartitionSpec as P


def per_device(w_gate, avg_gate, w_up, avg_up, mix_share, router_weight, router_gain):
    fresh_gate = mix_share[:, None, None] * w_gate + (1.0 - mix_share[:, None, None]) * avg_gate
    fresh_up = mix_share[:, None, None] * w_up + (1.0 - mix_share[:, None, None]) * avg_up
    total_gate, total_up = lax.psum(
        (jnp.sum(fresh_gate * fresh_gate, axis=1), jnp.sum(fresh_up * fresh_up, axis=1)), "shard"
    )
    scale_gate = jnp.sqrt(total_gate)
    scale_up = jnp.sqrt(total_up)
    narrow_gate, narrow_up = (
        (fresh_gate / jnp.expand_dims(scale_gate, 1)).astype(jnp.bfloat16),
        (fresh_up / jnp.expand_dims(scale_up, 1)).astype(jnp.bfloat16),
    )
    serve_gate, serve_up = (
        lax.all_gather(narrow_gate, "shard", axis=1, tiled=True),
        lax.all_gather(narrow_up, "shard", axis=1, tiled=True),
    )
    part_router = (router_weight * router_gain[:, None]).astype(jnp.bfloat16)
    row_router = lax.all_gather(part_router, "shard", axis=0, tiled=True)
    serve_router = lax.all_gather(row_router, "expert", axis=1, tiled=True)
    return (serve_gate, serve_up, scale_gate, scale_up, serve_router)


def solution(mesh):
    return jax.shard_map(
        per_device,
        mesh=mesh,
        in_specs=(
            P("expert", "shard", None),
            P("expert", "shard", None),
            P("expert", "shard", None),
            P("expert", "shard", None),
            P("expert"),
            P("shard", "expert"),
            P("shard"),
        ),
        out_specs=(
            P("expert", None, None),
            P("expert", None, None),
            P("expert", None),
            P("expert", None),
            P(),
        ),
        check_vma=False,
    )
```

profile of v0, /device:TPU:0, one launch (start us, length us, event | category | flops | bytes accessed | tf_op | source)
XLA Modules:
  0.0 1276.1 jit_solution(14333517205513151259)
XLA Ops:
  7.2 0.0 all-reduce.3.cloned.1.call-start
  7.2 0.7 broadcast_subtract_fusion
  7.9 0.0 copy-start.3
  7.9 23.3 %multiply_reduce_fusion = (f32[8,1024]{1,0:T(8,128)}, f32[8,1024]{1,0:T(8,128)}) fusion(f32[8,512,1024]{2,1,0:T(8,128)} %param.10, f32[8]{0:T(128)S(1)} %broadcast_subtract_fusion, f32[8,512,1024]{2,1,0:T(8,128)} %param.9, f32[8]{0:T(128)} %param.11, f32[8,512,1024]{2,1,0:T(8,128)} %param.8, f32[8,512,1024]{2,1,0:T(8,128)} %param.7), kind=kLoop, calls=%fused_computation.1 | loop fusion | flops 41926656 | bytes 67174464 | tf_op jit(solution)/shard_map/reduce_sum | solution.py:11
  31.1 0.0 all-reduce.3.cloned.1.call-update
  31.2 0.0 all-gather.3.cloned.1.call-start
  31.2 37.2 %all-reduce.3.cloned.1.call-done = (f32[8,1024]{1,0:T(8,128)}, f32[8,1024]{1,0:T(8,128)}) async-done(((f32[8,1024]{1,0:T(8,128)}, f32[8,1024]{1,0:T(8,128)}), (f32[8,1024]{1,0:T(8,128)}, f32[8,1024]{1,0:T(8,128)})) %all-reduce.3.cloned.1.call-update) | async-done | bytes 65552 | tf_op jit(solution)/shard_map/psum | solution.py:10
  68.4 0.8 sqrt.6
  69.2 0.0 copy-start
  69.2 0.8 sqrt.7
  70.0 0.0 copy-done.3
  70.0 0.0 copy-start.1
  70.0 29.3 %divide_convert_fusion = (bf16[8,512,1024]{2,1,0:T(8,128)(2,1)}, bf16[8,512,1024]{2,1,0:T(8,128)(2,1)}) fusion(f32[8,1024]{1,0:T(8,128)S(1)} %sqrt.7, f32[8,512,1024]{2,1,0:T(8,128)} %param.10, f32[8]{0:T(128)S(1)} %broadcast_subtract_fusion, f32[8,512,1024]{2,1,0:T(8,128)} %param.9, f32[8]{0:T(128)S(1)} %copy-done.3, f32[8,1024]{1,0:T(8,128)S(1)} %sqrt.6, ...), kind=kLoop, calls=%fused_computation | loop fusion | flops 41943040 | bytes 83951680 | tf_op jit(solution)/shard_map/convert_element_type | solution.py:17
  99.3 0.0 copy-done
  99.4 0.0 copy-done.1
  99.4 0.0 copy-start.2
  99.4 0.0 copy-start.4
  99.4 0.0 all-gather.3.cloned.1.call-update
  99.4 0.0 all-gather.5.cloned.1.call-start
  99.5 0.7 all-gather.5.cloned.1.call-update
  100.1 0.0 copy-done.2
  100.2 0.0 copy-done.4
  100.2 13.1 %all_gather.14 = bf16[2048,8]{0,1:T(8,128)(2,1)S(1)} all-gather(bf16[512,8]{0,1:T(8,128)(2,1)S(1)} %multiply_convert_fusion), channel_id=1, replica_groups=mesh['expert'=8,'shard'=4] {'shard'}, dimensions={0}, use_global_device_ids=true | all-gather | bytes 40960 | tf_op jit(solution)/shard_map/all_gather | solution.py:24
  113.3 9.2 all_gather.15
  122.6 538.1 %all-gather.3.cloned.1.call-done = bf16[8,2048,1024]{2,1,0:T(8,128)(2,1)} async-done(((bf16[8,512,1024]{2,1,0:T(8,128)(2,1)}), bf16[8,2048,1024]{2,1,0:T(8,128)(2,1)}) %all-gather.3.cloned.1.call-update) | async-done | bytes 33554448 | tf_op jit(solution)/shard_map/all_gather | solution.py:20
  660.7 561.8 %all-gather.5.cloned.1.call-done = bf16[8,2048,1024]{2,1,0:T(8,128)(2,1)} async-done(((bf16[8,512,1024]{2,1,0:T(8,128)(2,1)}), bf16[8,2048,1024]{2,1,0:T(8,128)(2,1)}) %all-gather.5.cloned.1.call-update) | async-done | bytes 33554448 | tf_op jit(solution)/shard_map/all_gather | solution.py:21
  1222.4 23.2 %copy.17 = bf16[8,2048,1024]{2,1,0:T(8,128)(2,1)} copy(bf16[8,2048,1024]{2,1,0:T(8,128)(2,1)} %all-gather.3.cloned.1.call-done) | data formatting | bytes 67108864
  1245.7 23.2 %copy.18 = bf16[8,2048,1024]{2,1,0:T(8,128)(2,1)} copy(bf16[8,2048,1024]{2,1,0:T(8,128)(2,1)} %all-gather.5.cloned.1.call-done) | data formatting | bytes 67108864
  1268.9 0.7 copy.19
  (1 shorter events, 0.0 us)
Async XLA Ops:
  7.2 61.2 %all-reduce.3.cloned.1.call-start = ((), (), s32[]{:S(2)}) async-start(), calls=%async_computation.2 | async-start | bytes 131072 | tf_op jit(solution)/shard_map/psum | solution.py:10
  7.9 62.1 %copy-start.3 = (f32[8]{0:T(128)S(1)}, f32[8]{0:T(128)}, u32[]{:S(2)}) copy-start(f32[8]{0:T(128)} %param.11) | copy-start | bytes 100
  31.2 629.5 %all-gather.3.cloned.1.call-start = ((), (), s32[]{:S(2)}) async-start(), calls=%async_computation | async-start | bytes 41943040 | tf_op jit(solution)/shard_map/all_gather | solution.py:20
  69.2 30.2 %copy-start = (f32[8,1024]{1,0:T(8,128)}, f32[8,1024]{1,0:T(8,128)S(1)}, u32[]{:S(2)}) copy-start(f32[8,1024]{1,0:T(8,128)S(1)} %sqrt.6) | copy-start | bytes 98308
  70.0 29.4 %copy-start.1 = (f32[8,1024]{1,0:T(8,128)}, f32[8,1024]{1,0:T(8,128)S(1)}, u32[]{:S(2)}) copy-start(f32[8,1024]{1,0:T(8,128)S(1)} %sqrt.7) | copy-start | bytes 98308
  99.4 0.8 copy-start.2
  99.4 0.8 copy-start.4
  99.4 1123.0 %all-gather.5.cloned.1.call-start = ((), (), s32[]{:S(2)}) async-start(), calls=%async_computation.1 | async-start | bytes 41943040 | tf_op jit(solution)/shard_map/all_gather | solution.py:21
Sparse Core Ops, SparseCore 0:
  31.3 37.0 all-reduce.2
  99.5 561.0 all-gather.2
  662.8 559.5 all-gather.4
where the time goes:
time: 1280 us
  waiting for transfers between devices  1140 us (89%)
  other arithmetic  53.3 us (4%)
  local copies, waits for them, and re-layouts  48.7 us (4%)
  blocking collectives  22.4 us (2%)
  between operations  13.8 us (1%)
    all_gather x1, waiting for transfers between devices, per_device(): lax.all_gather(narrow_up, 'shard', axis=1, tiled=True)  562 us
    all_gather x1, waiting for transfers between devices, per_device(): lax.all_gather(narrow_gate, 'shard', axis=1, tiled=True)  538 us
    unnamed x13, local copies, waits for them, and re-layouts  47.2 us
    psum x1, waiting for transfers between devices, per_device(): lax.psum((jnp.sum(fresh_gate * fresh_gate, axis=1), jnp.sum(fresh_up * fr...  37.2 us
    convert_element_type x1, other arithmetic, per_device(): (fresh_up / jnp.expand_dims(scale_up, 1)).astype(jnp.bfloat16)  29.3 us
  transfers between devices with their start and end apart: 3, of which 3 were waited for; matrix products, arithmetic and copies ran while one was open for 0% of the time, Pallas kernels for 0%

commit v1 on v0

--- a/solution.py
+++ b/solution.py
@@ -18,7 +18,7 @@
     )
     serve_gate, serve_up = (
         lax.all_gather(narrow_gate, "shard", axis=1, tiled=True),
-        lax.all_gather(narrow_up, "shard", axis=1, tiled=True),
+        jnp.concatenate(lax.all_gather(narrow_up, "shard"), axis=1),
     )
     part_router = (router_weight * router_gain[:, None]).astype(jnp.bfloat16)
     row_router = lax.all_gather(part_router, "shard", axis=0, tiled=True)

time: 1280 us -> 1250 us (0.977)
  waiting for transfers between devices: 1140 us -> 1110 us
    reshape x0 -> x1, local copies, waits for them, and re-layouts: none -> 25.9 us  [per_device(): jnp.concatenate(lax.all_gather(narrow_up, 'shard'), axis=1)]
    all_gather x1, waiting for transfers between devices: 562 us -> 538 us  [per_device(): lax.all_gather(narrow_up, 'shard')]
    unnamed x13 -> x12, local copies, waits for them, and re-layouts: 47.2 us -> 24 us
  transfers between devices with their start and end apart: 3 -> 3, of which waited for: 3 -> 3; matrix products, arithmetic and copies ran while one was open for 0% -> 2% of each run, Pallas kernels for 0% -> 0%
where the time goes in v1:
time: 1250 us
  waiting for transfers between devices  1110 us (89%)
  other arithmetic  53.3 us (4%)
  local copies, waits for them, and re-layouts  51.4 us (4%)
  blocking collectives  22.4 us (2%)
  between operations  13.8 us (1%)
    all_gather x1, waiting for transfers between devices, per_device(): lax.all_gather(narrow_up, 'shard')  538 us
    all_gather x1, waiting for transfers between devices, per_device(): lax.all_gather(narrow_gate, 'shard', axis=1, tiled=True)  536 us
    psum x1, waiting for transfers between devices, per_device(): lax.psum((jnp.sum(fresh_gate * fresh_gate, axis=1), jnp.sum(fresh_up * fr...  37.2 us
    convert_element_type x1, other arithmetic, per_device(): (fresh_up / jnp.expand_dims(scale_up, 1)).astype(jnp.bfloat16)  29.3 us
    reshape x1, local copies, waits for them, and re-layouts, per_device(): jnp.concatenate(lax.all_gather(narrow_up, 'shard'), axis=1)  25.9 us
  transfers between devices with their start and end apart: 3, of which 3 were waited for; matrix products, arithmetic and copies ran while one was open for 2% of the time, Pallas kernels for 0%

profile of v1, /device:TPU:0, one launch (start us, length us, event | category | flops | bytes accessed | tf_op | source)
XLA Modules:
  0.0 1252.9 jit_solution(7858928339932058002)
XLA Ops:
  7.2 0.0 all-reduce.3.cloned.1.call-start
  7.2 0.7 broadcast_subtract_fusion
  7.9 0.0 copy-start.3
  7.9 23.3 %multiply_reduce_fusion = (f32[8,1024]{1,0:T(8,128)}, f32[8,1024]{1,0:T(8,128)}) fusion(f32[8,512,1024]{2,1,0:T(8,128)} %param.10, f32[8]{0:T(128)S(1)} %broadcast_subtract_fusion, f32[8,512,1024]{2,1,0:T(8,128)} %param.9, f32[8]{0:T(128)} %param.11, f32[8,512,1024]{2,1,0:T(8,128)} %param.8, f32[8,512,1024]{2,1,0:T(8,128)} %param.7), kind=kLoop, calls=%fused_computation.1 | loop fusion | flops 41926656 | bytes 67174464 | tf_op jit(solution)/shard_map/reduce_sum | solution.py:11
  31.1 0.0 all-reduce.3.cloned.1.call-update
  31.2 0.0 all-gather.6.cloned.1.call-start
  31.2 37.2 %all-reduce.3.cloned.1.call-done = (f32[8,1024]{1,0:T(8,128)}, f32[8,1024]{1,0:T(8,128)}) async-done(((f32[8,1024]{1,0:T(8,128)}, f32[8,1024]{1,0:T(8,128)}), (f32[8,1024]{1,0:T(8,128)}, f32[8,1024]{1,0:T(8,128)})) %all-reduce.3.cloned.1.call-update) | async-done | bytes 65552 | tf_op jit(solution)/shard_map/psum | solution.py:10
  68.4 0.8 sqrt.6
  69.2 0.0 copy-start
  69.2 0.8 sqrt.7
  70.0 0.0 copy-done.3
  70.0 0.0 copy-start.1
  70.0 29.3 %divide_convert_fusion = (bf16[8,512,1024]{2,1,0:T(8,128)(2,1)}, bf16[8,512,1024]{2,1,0:T(8,128)(2,1)}) fusion(f32[8,1024]{1,0:T(8,128)S(1)} %sqrt.7, f32[8,512,1024]{2,1,0:T(8,128)} %param.10, f32[8]{0:T(128)S(1)} %broadcast_subtract_fusion, f32[8,512,1024]{2,1,0:T(8,128)} %param.9, f32[8]{0:T(128)S(1)} %copy-done.3, f32[8,1024]{1,0:T(8,128)S(1)} %sqrt.6, ...), kind=kLoop, calls=%fused_computation | loop fusion | flops 41943040 | bytes 83951680 | tf_op jit(solution)/shard_map/convert_element_type | solution.py:17
  99.3 0.0 copy-done
  99.4 0.0 copy-done.1
  99.4 0.0 copy-start.2
  99.4 0.0 copy-start.4
  99.4 0.0 all-gather.6.cloned.1.call-update
  99.4 0.0 all-gather.4.cloned.1.call-start
  99.5 0.7 all-gather.4.cloned.1.call-update
  100.1 0.0 copy-done.2
  100.2 0.0 copy-done.4
  100.2 13.1 %all_gather.18 = bf16[2048,8]{0,1:T(8,128)(2,1)S(1)} all-gather(bf16[512,8]{0,1:T(8,128)(2,1)S(1)} %multiply_convert_fusion), channel_id=1, replica_groups=mesh['expert'=8,'shard'=4] {'shard'}, dimensions={0}, use_global_device_ids=true | all-gather | bytes 40960 | tf_op jit(solution)/shard_map/all_gather | solution.py:24
  113.3 9.2 all_gather.19
  122.6 538.1 %all-gather.6.cloned.1.call-done = bf16[32,512,1024]{2,1,0:T(8,128)(2,1)} async-done(((bf16[8,512,1024]{2,1,0:T(8,128)(2,1)}), bf16[32,512,1024]{2,1,0:T(8,128)(2,1)}) %all-gather.6.cloned.1.call-update) | async-done | bytes 33554448 | tf_op jit(solution)/shard_map/all_gather | solution.py:21
  660.7 25.9 %copy.13 = bf16[8,4,512,1024]{3,2,1,0:T(8,128)(2,1)} copy(bf16[8,4,512,1024]{3,2,0,1:T(8,128)(2,1)} %bitcast.4) | data formatting | bytes 67108864 | tf_op jit(solution)/shard_map/reshape | solution.py:21
  686.6 535.8 %all-gather.4.cloned.1.call-done = bf16[8,2048,1024]{2,1,0:T(8,128)(2,1)} async-done(((bf16[8,512,1024]{2,1,0:T(8,128)(2,1)}), bf16[8,2048,1024]{2,1,0:T(8,128)(2,1)}) %all-gather.4.cloned.1.call-update) | async-done | bytes 33554448 | tf_op jit(solution)/shard_map/all_gather | solution.py:20
  1222.4 23.2 %copy.18 = bf16[8,2048,1024]{2,1,0:T(8,128)(2,1)} copy(bf16[8,2048,1024]{2,1,0:T(8,128)(2,1)} %all-gather.4.cloned.1.call-done) | data formatting | bytes 67108864
  1245.6 0.7 copy.19
  (1 shorter events, 0.0 us)
Async XLA Ops:
  7.2 61.2 %all-reduce.3.cloned.1.call-start = ((), (), s32[]{:S(2)}) async-start(), calls=%async_computation.2 | async-start | bytes 131072 | tf_op jit(solution)/shard_map/psum | solution.py:10
  7.9 62.1 %copy-start.3 = (f32[8]{0:T(128)S(1)}, f32[8]{0:T(128)}, u32[]{:S(2)}) copy-start(f32[8]{0:T(128)} %param.11) | copy-start | bytes 100
  31.2 629.5 %all-gather.6.cloned.1.call-start = ((), (), s32[]{:S(2)}) async-start(), calls=%async_computation.1 | async-start | bytes 41943040 | tf_op jit(solution)/shard_map/all_gather | solution.py:21
  69.2 30.2 %copy-start = (f32[8,1024]{1,0:T(8,128)}, f32[8,1024]{1,0:T(8,128)S(1)}, u32[]{:S(2)}) copy-start(f32[8,1024]{1,0:T(8,128)S(1)} %sqrt.6) | copy-start | bytes 98308
  70.0 29.4 %copy-start.1 = (f32[8,1024]{1,0:T(8,128)}, f32[8,1024]{1,0:T(8,128)S(1)}, u32[]{:S(2)}) copy-start(f32[8,1024]{1,0:T(8,128)S(1)} %sqrt.7) | copy-start | bytes 98308
  99.4 0.8 copy-start.2
  99.4 0.8 copy-start.4
  99.4 1123.0 %all-gather.4.cloned.1.call-start = ((), (), s32[]{:S(2)}) async-start(), calls=%async_computation | async-start | bytes 41943040 | tf_op jit(solution)/shard_map/all_gather | solution.py:20
Sparse Core Ops, SparseCore 0:
  31.3 37.0 all-reduce.2
  99.5 561.0 all-gather.5
  662.8 559.5 all-gather.3
